TPU v7x, 32 devices: a whole 2x2x4 slice. The times are simulated.
32 devices in a mesh: layer: 4 (over x, core), harm: 8 (over z, y).
Axes of the slice: x: 2, y: 2, z: 4, core: 2. Of those that a mesh axis runs over, the one named last changes fastest.
Arguments:
- source: bfloat16 [2, 2048, 128], P(None, 'harm'), may hold values from -6 to 6
- transfer: bfloat16 [4, 2, 2048, 2048], P('layer', None, 'harm'), may hold values from -0.09375 to 0.09375
- fields: bfloat16 [4, 2, 2048, 128], P('layer', None, 'harm'), may hold values from -6 to 6
- orders: int32 [2048], replicated, may hold values from 0 to 2047, each once
Outputs:
- gradients: float32 [4, 2, 4096], P('layer', None, 'harm')
- boundary: bfloat16 [4, 2, 2048, 128], P('layer', None, 'harm')
Inputs may be any that keep to these rules, and one draw needn't show every extreme that they name: `orders`: every value from 0 to 2047 appears exactly once.
All inputs are finite; a program needn't handle non-finite values.
Results may differ from a plain program's by a relative error of at most 0.006.
Values may be sent and summed in bfloat16 or wider, within the bound.
A program may use at most 64 MiB of HBM per device.

v0:
```python
import functools
import math

import jax
import jax.numpy as jnp
from jax import lax
from jax.experimental import pallas as pl
from jax.experimental.pallas import tpu as pltpu
from jax.sharding import PartitionSpec as P

MESH = pl.DeviceIdType.MESH


def flipped(index, bits, count):
    total = 0
    place = 1
    while place < count:
        digit = (index // place) % 2
        total = total + (1 - digit if (bits // place) % 2 else digit) * place
        place *= 2
    return total


def sweep_kernel(
    sections,
    members,
    inner,
    block,
    source_ref,
    transfer_ref,
    fields_ref,
    orders_ref,
    grads_ref,
    bottom_ref,
    matrix,
    adj,
    fwd,
    out_block,
    onehot,
    left,
    padded,
    local_sems,
    adj_recv,
    fwd_recv,
    adj_send,
    adj_forward,
    down_send,
    fwd_send,
    fwd_forward,
):
    outer = members // inner
    section = lax.axis_index("layer")
    member = lax.axis_index("harm")
    o_index, i_index = member // inner, member % inner
    rows = out_block.shape[0]
    harmonics = adj.shape[0]
    columns = adj.shape[1] // 2
    band = 2 * harmonics // members
    width = block + band
    top = section == sections - 1
    early = section < sections // 2

    def rows_of(index):
        return pl.ds(pl.multiple_of(index * rows, rows), rows)

    load_matrix = pltpu.make_async_copy(transfer_ref.at[0], matrix, local_sems.at[0])
    load_matrix.start()
    loads = []
    for part in range(2):
        lanes = pl.ds(part * columns, columns)
        loads.append(
            pltpu.make_async_copy(fields_ref.at[0, part], fwd.at[rows_of(member), lanes], local_sems.at[1 + part])
        )
        loads.append(
            pltpu.make_async_copy(source_ref.at[part], adj.at[rows_of(member), lanes], local_sems.at[3 + part])
        )
    loads[0].start()
    loads[2].start()

    @pl.when(top)
    def _():
        loads[1].start()
        loads[3].start()

    barrier = pltpu.get_barrier_semaphore()
    peers = [(section, flipped(o_index, t, outer) * inner + i_index) for t in range(1, outer)]
    peers += [(section, o_index * inner + flipped(i_index, u, inner)) for u in range(1, inner)]
    for step in (1, sections - 1):
        peers += [((section + step) % sections, flipped(o_index, t, outer) * inner + i_index) for t in range(outer)]
    for peer in peers:
        pl.semaphore_signal(barrier, inc=1, device_id=peer, device_id_type=MESH)
    padded[: harmonics, :] = jnp.zeros((harmonics, 2 * columns), padded.dtype)
    padded[2 * harmonics :, :] = jnp.zeros((harmonics, 2 * columns), padded.dtype)
    loads[0].wait()
    loads[2].wait()

    @pl.when(top)
    def _():
        loads[1].wait()
        loads[3].wait()

    pl.semaphore_wait(barrier, len(peers))

    def line_copy(buffer, send, recv, t):
        target = flipped(o_index, t, outer) * inner + i_index
        return pltpu.make_async_remote_copy(
            src_ref=buffer.at[rows_of(member)],
            dst_ref=buffer.at[rows_of(member)],
            send_sem=send.at[t],
            recv_sem=recv.at[member],
            device_id=(section, target),
            device_id_type=MESH,
        )

    def down_copy(t):
        target = flipped(o_index, t, outer) * inner + i_index
        return pltpu.make_async_remote_copy(
            src_ref=out_block,
            dst_ref=adj.at[rows_of(member)],
            send_sem=down_send.at[t],
            recv_sem=adj_recv.at[member],
            device_id=(section - 1, target),
            device_id_type=MESH,
        )

    def forward_copy(buffer, send, recv, t, u):
        held = flipped(o_index, t, outer) * inner + i_index
        target = o_index * inner + flipped(i_index, u, inner)
        return pltpu.make_async_remote_copy(
            src_ref=buffer.at[rows_of(held)],
            dst_ref=buffer.at[rows_of(held)],
            send_sem=send.at[t, u],
            recv_sem=recv.at[held],
            device_id=(section, target),
            device_id_type=MESH,
        )

    def arrival(buffer, recv, index):
        return pltpu.make_async_remote_copy(
            src_ref=buffer.at[rows_of(index)],
            dst_ref=buffer.at[rows_of(index)],
            send_sem=recv.at[index],
            recv_sem=recv.at[index],
            device_id=(section, index),
            device_id_type=MESH,
        )

    def start_line(buffer, send, recv):
        for t in range(1, outer):
            line_copy(buffer, send, recv, t).start()

    def relay(buffer, recv, forward, t):
        for u in range(1, inner):
            forward_copy(buffer, forward, recv, t, u).start()

    def collect(buffer, recv, forward, own_here):
        for t in range(outer):
            held = flipped(o_index, t, outer) * inner + i_index
            if t == 0 and own_here is True:
                pass
            elif t == 0 and own_here is not False:

                @pl.when(jnp.logical_not(own_here))
                def _():
                    arrival(buffer, recv, held).wait_recv()
            else:
                arrival(buffer, recv, held).wait_recv()
            relay(buffer, recv, forward, t)
        for t in range(outer):
            for u in range(1, inner):
                held = flipped(o_index, t, outer) * inner + flipped(i_index, u, inner)
                arrival(buffer, recv, held).wait_recv()

    def finish_forwards(buffer, recv, forward):
        for t in range(outer):
            for u in range(1, inner):
                forward_copy(buffer, forward, recv, t, u).wait_send()

    def finish_line(buffer, send, recv):
        for t in range(1, outer):
            line_copy(buffer, send, recv, t).wait_send()

    def gather_fields():
        start_line(fwd, fwd_send, fwd_recv)
        collect(fwd, fwd_recv, fwd_forward, True)

    def build_onehot(reverse):
        tile = block

        @pl.loop(0, harmonics // tile)
        def _(index):
            start = pl.multiple_of(index * tile, tile)
            line = lax.broadcasted_iota(jnp.int32, (tile, harmonics), 0)
            wanted = start + (tile - 1 - line if reverse else line)
            onehot[pl.ds(start, tile), :] = jnp.where(orders_ref[...] == wanted, 1.0, 0.0).astype(onehot.dtype)

    def sort_fields():
        build_onehot(True)

        @pl.loop(0, harmonics // block)
        def _(index):
            start = pl.multiple_of(index * block, block)
            sorted_rows = jnp.dot(onehot[pl.ds(start, block), :], fwd[...], preferred_element_type=jnp.float32)
            real, imag = sorted_rows[:, :columns], sorted_rows[:, columns:]
            left[index, :block, :] = jnp.concatenate([real, -imag], axis=1).astype(left.dtype)
            left[index, block:, :] = jnp.concatenate([imag, real], axis=1).astype(left.dtype)

        build_onehot(False)

    @pl.when(early)
    def _():
        gather_fields()
        sort_fields()

    @pl.when(top)
    def _():
        start_line(adj, adj_send, adj_recv)

    load_matrix.wait()
    collect(adj, adj_recv, adj_forward, top)

    by_real = jnp.dot(matrix[0], adj[...], preferred_element_type=jnp.float32)
    by_imag = jnp.dot(matrix[1], adj[...], preferred_element_type=jnp.float32)
    result = jnp.concatenate(
        [by_real[:, :columns] - by_imag[:, columns:], by_real[:, columns:] + by_imag[:, :columns]], axis=1
    ).astype(out_block.dtype)
    out_block[...] = result
    bottom_ref[...] = result

    @pl.when(section > 0)
    def _():
        for t in range(outer):
            down_copy(t).start()

    @pl.when(jnp.logical_not(early))
    def _():
        gather_fields()
        sort_fields()

    tile = 2 * block if harmonics % (2 * block) == 0 else block

    @pl.loop(0, harmonics // tile)
    def _(index):
        start = pl.multiple_of(index * tile, tile)
        padded[pl.ds(pl.multiple_of(harmonics + start, tile), tile), :] = jnp.dot(
            onehot[pl.ds(start, tile), :], adj[...], preferred_element_type=jnp.float32
        ).astype(padded.dtype)

    total = jnp.zeros((2 * block, width), jnp.float32)
    for index in range(harmonics // block):
        window = padded[pl.ds(pl.multiple_of(member * band + index * block, block), width), :]
        total = total + lax.dot_general(
            left[index], window, (((1,), (1,)), ((), ())), preferred_element_type=jnp.float32
        )
    for part in range(2):
        rolled = pltpu.roll(
            total[part * block : (part + 1) * block], width - block, 1, stride=1, stride_axis=0
        )
        grads_ref[part : part + 1, :] = jnp.sum(rolled, axis=0, keepdims=True)[:, :band]

    finish_forwards(adj, adj_recv, adj_forward)
    finish_line(fwd, fwd_send, fwd_recv)
    finish_forwards(fwd, fwd_recv, fwd_forward)

    @pl.when(top)
    def _():
        finish_line(adj, adj_send, adj_recv)

    @pl.when(section > 0)
    def _():
        for t in range(outer):
            down_copy(t).wait_send()


def per_device(source, transfer, fields, orders):
    harmonics = orders.shape[0]
    sections = lax.axis_size("layer")
    members = lax.axis_size("harm")
    rows = transfer.shape[2]
    columns = source.shape[2]
    inner = 1 << ((members.bit_length() - 1) // 2)
    outer = members // inner
    band = 2 * harmonics // members
    block = min(128, band)
    norm_scale = 1.0 / math.sqrt(harmonics * columns)
    any_space = pl.BlockSpec(memory_space=pl.ANY)
    vmem = pl.BlockSpec(memory_space=pltpu.VMEM)
    dma = pltpu.SemaphoreType.DMA
    grads, bottom = pl.pallas_call(
        functools.partial(sweep_kernel, sections, members, inner, block),
        out_shape=(
            jax.ShapeDtypeStruct((2, band), jnp.float32),
            jax.ShapeDtypeStruct((rows, 2 * columns), jnp.bfloat16),
        ),
        in_specs=[any_space, any_space, any_space, vmem],
        out_specs=(vmem, vmem),
        scratch_shapes=[
            pltpu.VMEM((2, rows, harmonics), jnp.bfloat16),
            pltpu.VMEM((harmonics, 2 * columns), jnp.bfloat16),
            pltpu.VMEM((harmonics, 2 * columns), jnp.bfloat16),
            pltpu.VMEM((rows, 2 * columns), jnp.bfloat16),
            pltpu.VMEM((harmonics, harmonics), jnp.bfloat16),
            pltpu.VMEM((harmonics // block, 2 * block, 2 * columns), jnp.bfloat16),
            pltpu.VMEM((3 * harmonics, 2 * columns), jnp.bfloat16),
            dma((5,)),
            dma((members,)),
            dma((members,)),
            dma((outer,)),
            dma((outer, inner)),
            dma((outer,)),
            dma((outer,)),
            dma((outer, inner)),
        ],
        compiler_params=pltpu.CompilerParams(collective_id=0, has_side_effects=True),
        name="sweep",
    )(source, transfer, fields, orders.reshape(1, harmonics))
    boundary = jnp.stack([bottom[:, :columns], bottom[:, columns:]])[None]
    return (grads * norm_scale)[None], boundary


def solution(mesh):
    return jax.shard_map(
        per_device,
        mesh=mesh,
        in_specs=(
            P(None, "harm", None),
            P("layer", None, "harm", None),
            P("layer", None, "harm", None),
            P(),
        ),
        out_specs=(P("layer", None, "harm"), P("layer", None, "harm", None)),
        check_vma=False,
    )
```

profile of v0, /device:TPU:0, one launch (start us, length us, event | category | flops | bytes accessed | tf_op | source)
XLA Modules:
  0.0 68.4 jit_solution(1400673132672272773)
XLA Ops:
  0.6 65.0 %sweep.1 = (f32[2,512]{1,0:T(2,128)}, bf16[256,256]{1,0:T(8,128)(2,1)}) custom-call(bf16[2,256,128]{2,1,0:T(8,128)(2,1)} %source_ref.1, bf16[1,2,256,2048]{3,2,1,0:T(8,128)(2,1)} %transfer_ref.1, bf16[1,2,256,128]{3,2,1,0:T(8,128)(2,1)} %fields_ref.1, s32[1,2048]{1,0:T(1,128)} %bitcast.9), custom_call_target="tpu_custom_call" | custom-call | tf_op jit(solution)/shard_map/sweep/pallas_call | solution.py:289
  65.6 1.3 %multiply_bitcast_fusion = f32[1,2,512]{2,1,0:T(2,128)} fusion(f32[2,512]{1,0:T(2,128)} %get-tuple-element.4), kind=kLoop, calls=%fused_computation.3 | loop fusion | flops 1024 | bytes 8192 | tf_op jit(solution)/shard_map/broadcast_in_dim | solution.py:318
  66.9 0.9 %slice_bitcast_fusion.1 = (bf16[1,256,128]{2,1,0:T(8,128)(2,1)S(1)}, bf16[1,256,128]{2,1,0:T(8,128)(2,1)S(1)}) fusion(bf16[256,256]{1,0:T(8,128)(2,1)} %get-tuple-element.5), kind=kLoop, calls=%fused_computation.2 | loop fusion | bytes 262144 | tf_op jit(solution)/shard_map/stack | solution.py:317
  67.8 0.7 maximum_bitcast_fusion
where the time goes:
time: 68.7 us; the launch traced here: 68.4 us
  Pallas kernels  65 us (95%)
  other arithmetic  1.94 us (3%)
  local copies, waits for them, and re-layouts  0.88 us (1%)
    pallas_call x1, Pallas kernels, per_device(): pl.pallas_call(functools.partial(sweep_kernel, sections, members, inner,...  65 us

commit v1 on v0

v1 whole, which is shorter than its diff:
```python
import functools
import math

import jax
import jax.numpy as jnp
from jax import lax
from jax.experimental import pallas as pl
from jax.experimental.pallas import tpu as pltpu
from jax.sharding import PartitionSpec as P

MESH = pl.DeviceIdType.MESH
REACH = 3
CROSS = (0,)
FAR_FIRST = False


def flipped(index, bits, count):
    total = 0
    place = 1
    while place < count:
        digit = (index // place) % 2
        total = total + (1 - digit if (bits // place) % 2 else digit) * place
        place *= 2
    return total


def guarded(condition, action):
    if condition is None:
        action()
    else:
        pl.when(condition)(action)


def sweep_kernel(
    sections,
    members,
    inner,
    block,
    source_ref,
    transfer_ref,
    fields_ref,
    orders_ref,
    grads_ref,
    bottom_ref,
    matrix,
    staged,
    adj,
    fwd,
    out_block,
    onehot_adj,
    onehot_fwd,
    left,
    padded,
    local_sems,
    go_sem,
    adj_recv,
    adj_send,
    adj_relay,
    adj_forward,
    down_send,
    fwd_recv,
    fwd_send,
    fwd_relay,
    fwd_forward,
):
    outer = members // inner
    section = lax.axis_index("layer")
    member = lax.axis_index("harm")
    o_index, i_index = member // inner, member % inner
    rows = out_block.shape[0]
    harmonics = adj.shape[0]
    columns = adj.shape[1] // 2
    chunks = adj_recv.shape[0]
    lanes = adj.shape[1] // chunks
    half = lanes // 2
    band = 2 * harmonics // members
    width = block + band
    top = section == sections - 1
    early = section < sections // 2
    reach = min(REACH, outer - 1)
    near = sorted(range(1 - outer, outer), key=abs)
    order = sorted(range(-reach, reach + 1), key=abs, reverse=FAR_FIRST)

    def rows_of(index):
        return pl.ds(pl.multiple_of(index * rows, rows), rows)

    load_matrix = pltpu.make_async_copy(transfer_ref.at[0], matrix, local_sems.at[0])
    load_source = pltpu.make_async_copy(source_ref, staged, local_sems.at[1])
    load_fields = [
        pltpu.make_async_copy(
            fields_ref.at[0, part], fwd.at[rows_of(member), pl.ds(part * columns, columns)], local_sems.at[2 + part]
        )
        for part in range(2)
    ]
    load_source.start()
    load_matrix.start()
    for load in load_fields:
        load.start()

    barrier = pltpu.get_barrier_semaphore()
    peers = [(section, flipped(member, t, members)) for t in range(1, members)]
    for step in (1, sections - 1):
        peers += [((section + step) % sections, flipped(member, t, members)) for t in range(members)]
    for peer in peers:
        pl.semaphore_signal(barrier, inc=1, device_id=peer, device_id_type=MESH)
    load_source.wait()

    @pl.when(top)
    def _():
        for m in range(chunks):
            span = slice(m * half, (m + 1) * half)
            adj[rows_of(member), m * lanes : (m + 1) * lanes] = jnp.concatenate(
                [staged[0][:, span], staged[1][:, span]], axis=1
            )

    pl.semaphore_wait(barrier, len(peers))

    def present(d):
        return None if d == 0 else jnp.logical_and(o_index + d >= 0, o_index + d < outer)

    def lanes_of(buffer, recv, m):
        size = buffer.shape[1] // recv.shape[0]
        return pl.ds(m * size, size)

    def line_copy(buffer, send, recv, m, d, u, own_section=True):
        span = lanes_of(buffer, recv, m)
        return pltpu.make_async_remote_copy(
            src_ref=buffer.at[rows_of(member), span] if own_section else out_block.at[:, span],
            dst_ref=buffer.at[rows_of(member), span],
            send_sem=send.at[m, d + reach, u],
            recv_sem=recv.at[m, member],
            device_id=(section if own_section else section - 1, (o_index + d) * inner + flipped(i_index, u, inner)),
            device_id_type=MESH,
        )

    def forward_copy(buffer, send, recv, m, d, u):
        span = lanes_of(buffer, recv, m)
        held = member - d * inner
        return pltpu.make_async_remote_copy(
            src_ref=buffer.at[rows_of(held), span],
            dst_ref=buffer.at[rows_of(held), span],
            send_sem=send.at[m, d + outer - 1, u],
            recv_sem=recv.at[m, held],
            device_id=(section, o_index * inner + flipped(i_index, u, inner)),
            device_id_type=MESH,
        )

    def relay_copy(buffer, send, recv, m, d):
        span = lanes_of(buffer, recv, m)
        held = member - d * inner
        return pltpu.make_async_remote_copy(
            src_ref=buffer.at[rows_of(held), span],
            dst_ref=buffer.at[rows_of(held), span],
            send_sem=send.at[m, d + outer - 1],
            recv_sem=recv.at[m, held],
            device_id=(section, member + (inner if d > 0 else -inner)),
            device_id_type=MESH,
        )

    def relays(d):
        return reach <= abs(d) < outer - 1

    def onward(d):
        step = 1 if d > 0 else -1
        return jnp.logical_and(o_index + step >= 0, o_index + step < outer)

    def arrival(buffer, recv, m, index):
        span = lanes_of(buffer, recv, m)
        return pltpu.make_async_remote_copy(
            src_ref=buffer.at[rows_of(index), span],
            dst_ref=buffer.at[rows_of(index), span],
            send_sem=recv.at[m, index],
            recv_sem=recv.at[m, index],
            device_id=(section, index),
            device_id_type=MESH,
        )

    def each_line(buffer, send, recv, m, finish=False, own_section=True):
        for d in order:
            for u in range(inner if abs(d) in CROSS else 1):
                if own_section and d == 0 and u == 0:
                    continue
                copy = line_copy(buffer, send, recv, m, d, u, own_section)
                guarded(present(d), copy.wait_send if finish else copy.start)

    def each_down(m, finish=False):
        each_line(adj, down_send, adj_recv, m, finish, own_section=False)

    def pass_on(buffer, recv, relay, forward, m, d, finish=False):
        if relays(d):
            copy = relay_copy(buffer, relay, recv, m, d)
            guarded(onward(d), copy.wait_send if finish else copy.start)
        for u in range(1, inner if abs(d) not in CROSS else 1):
            copy = forward_copy(buffer, forward, recv, m, d, u)
            if finish:
                copy.wait_send()
            else:
                copy.start()

    def collect_line(buffer, recv, relay, forward, m, own_here):
        for d in near:

            def step(d=d):
                if d == 0 and own_here is None:
                    pass
                elif d == 0:
                    pl.when(jnp.logical_not(own_here))(arrival(buffer, recv, m, member).wait_recv)
                else:
                    arrival(buffer, recv, m, member - d * inner).wait_recv()
                pass_on(buffer, recv, relay, forward, m, d)

            guarded(present(-d), step)

    def collect_inner(buffer, recv, m):
        for t in range(outer):
            for u in range(1, inner):
                held = flipped(o_index, t, outer) * inner + flipped(i_index, u, inner)
                arrival(buffer, recv, m, held).wait_recv()

    def finish_passing(buffer, recv, relay, forward, m):
        for d in near:
            guarded(present(-d), functools.partial(pass_on, buffer, recv, relay, forward, m, d, finish=True))

    def start_fields():
        for m in range(fwd_recv.shape[0]):
            each_line(fwd, fwd_send, fwd_recv, m)

    def relay_fields():
        for m in range(fwd_recv.shape[0]):
            collect_line(fwd, fwd_recv, fwd_relay, fwd_forward, m, None)

    def finish_fields():
        for m in range(fwd_recv.shape[0]):
            collect_inner(fwd, fwd_recv, m)

    def build_onehots():
        @pl.loop(0, harmonics // block)
        def _(index):
            start = pl.multiple_of(index * block, block)
            line = lax.broadcasted_iota(jnp.int32, (block, harmonics), 0)
            orders = orders_ref[...].reshape(1, harmonics) - start
            dtype = onehot_adj.dtype
            onehot_adj[pl.ds(start, block), :] = jnp.where(orders == line, 1.0, 0.0).astype(dtype)
            onehot_fwd[pl.ds(start, block), :] = jnp.where(orders == block - 1 - line, 1.0, 0.0).astype(dtype)

        padded[:harmonics, :] = jnp.zeros((harmonics, 2 * columns), padded.dtype)
        padded[2 * harmonics :, :] = jnp.zeros((harmonics, 2 * columns), padded.dtype)

    def sort_fields():
        @pl.loop(0, harmonics // block)
        def _(index):
            start = pl.multiple_of(index * block, block)
            sorted_rows = jnp.dot(onehot_fwd[pl.ds(start, block), :], fwd[...], preferred_element_type=jnp.float32)
            real, imag = sorted_rows[:, :columns], sorted_rows[:, columns:]
            for_real, for_imag = [], []
            for m in range(chunks):
                span = slice(m * half, (m + 1) * half)
                for_real += [real[:, span], -imag[:, span]]
                for_imag += [imag[:, span], real[:, span]]
            left[index, :block, :] = jnp.concatenate(for_real, axis=1).astype(left.dtype)
            left[index, block:, :] = jnp.concatenate(for_imag, axis=1).astype(left.dtype)

    tile = 2 * block if harmonics % (2 * block) == 0 else block

    def sort_adjoint():
        @pl.loop(0, harmonics // tile)
        def _(index):
            start = pl.multiple_of(index * tile, tile)
            padded[pl.ds(pl.multiple_of(harmonics + start, tile), tile), :] = jnp.dot(
                onehot_adj[pl.ds(start, tile), :], adj[...], preferred_element_type=jnp.float32
            ).astype(padded.dtype)

    @pl.when(top)
    def _():
        for m in range(chunks):
            each_line(adj, adj_send, adj_recv, m)

    for load in load_fields:
        load.wait()

    @pl.when(jnp.logical_not(early) & jnp.logical_not(top))
    def _():
        build_onehots()

    @pl.when(section < sections // 2 - 1)
    def _():
        build_onehots()
        pl.semaphore_wait(go_sem, 1)

    @pl.when(early)
    def _():
        start_fields()

    @pl.when(section == sections // 2 - 1)
    def _():
        build_onehots()

    @pl.when(early)
    def _():
        relay_fields()
        finish_fields()

    @pl.when(early & (section > 0))
    def _():
        pl.semaphore_signal(go_sem, inc=1, device_id=(section - 1, member), device_id_type=MESH)

    @pl.when(early)
    def _():
        sort_fields()

    load_matrix.wait()
    for m in range(chunks):
        collect_line(adj, adj_recv, adj_relay, adj_forward, m, top)
    results = []
    for m in range(chunks):
        collect_inner(adj, adj_recv, m)
        values = adj[:, m * lanes : (m + 1) * lanes]
        by_real = jnp.dot(matrix[0], values, preferred_element_type=jnp.float32)
        by_imag = jnp.dot(matrix[1], values, preferred_element_type=jnp.float32)
        real = by_real[:, :half] - by_imag[:, half:]
        imag = by_real[:, half:] + by_imag[:, :half]
        out_block[:, m * lanes : (m + 1) * lanes] = jnp.concatenate([real, imag], axis=1).astype(out_block.dtype)

        @pl.when(section > 0)
        def _(m=m):
            each_down(m)

    for part in range(2):
        pieces = [out_block[:, m * lanes + part * half : m * lanes + (part + 1) * half] for m in range(chunks)]
        bottom_ref[part] = jnp.concatenate(pieces, axis=1)

    @pl.when(jnp.logical_and(jnp.logical_not(early), jnp.logical_not(top)))
    def _():
        pl.semaphore_signal(go_sem, inc=1, device_id=(section + 1, member), device_id_type=MESH)

    @pl.when(top)
    def _():
        build_onehots()

    @pl.when(section > sections // 2)
    def _():
        pl.semaphore_wait(go_sem, 1)

    @pl.when(jnp.logical_not(early))
    def _():
        start_fields()
        relay_fields()
        sort_adjoint()
        finish_fields()
        sort_fields()

    @pl.when(early)
    def _():
        sort_adjoint()

    total = jnp.zeros((2 * block, width), jnp.float32)
    for index in range(harmonics // block):
        window = padded[pl.ds(pl.multiple_of(member * band + index * block, block), width), :]
        total = total + lax.dot_general(
            left[index], window, (((1,), (1,)), ((), ())), preferred_element_type=jnp.float32
        )
    for part in range(2):
        rolled = pltpu.roll(
            total[part * block : (part + 1) * block], width - block, 1, stride=1, stride_axis=0
        )
        grads_ref[part : part + 1, :] = jnp.sum(rolled, axis=0, keepdims=True)[:, :band]

    for m in range(chunks):
        finish_passing(adj, adj_recv, adj_relay, adj_forward, m)
    for m in range(fwd_recv.shape[0]):
        each_line(fwd, fwd_send, fwd_recv, m, finish=True)
        finish_passing(fwd, fwd_recv, fwd_relay, fwd_forward, m)

    @pl.when(top)
    def _():
        for m in range(chunks):
            each_line(adj, adj_send, adj_recv, m, finish=True)

    @pl.when(section > 0)
    def _():
        for m in range(chunks):
            each_down(m, finish=True)


def per_device(source, transfer, fields, orders):
    harmonics = orders.shape[0]
    sections = lax.axis_size("layer")
    members = lax.axis_size("harm")
    rows = transfer.shape[2]
    columns = source.shape[2]
    inner = 1 << ((members.bit_length() - 1) // 2)
    outer = members // inner
    band = 2 * harmonics // members
    block = min(128, band)
    chunks = max(1, 2 * columns // 128)
    reach = min(REACH, outer - 1)
    norm_scale = 1.0 / math.sqrt(harmonics * columns)
    any_space = pl.BlockSpec(memory_space=pl.ANY)
    vmem = pl.BlockSpec(memory_space=pltpu.VMEM)
    dma = pltpu.SemaphoreType.DMA
    grads, bottom = pl.pallas_call(
        functools.partial(sweep_kernel, sections, members, inner, block),
        out_shape=(
            jax.ShapeDtypeStruct((2, band), jnp.float32),
            jax.ShapeDtypeStruct((2, rows, columns), jnp.bfloat16),
        ),
        in_specs=[any_space, any_space, any_space, vmem],
        out_specs=(vmem, vmem),
        scratch_shapes=[
            pltpu.VMEM((2, rows, harmonics), jnp.bfloat16),
            pltpu.VMEM((2, rows, columns), jnp.bfloat16),
            pltpu.VMEM((harmonics, 2 * columns), jnp.bfloat16),
            pltpu.VMEM((harmonics, 2 * columns), jnp.bfloat16),
            pltpu.VMEM((rows, 2 * columns), jnp.bfloat16),
            pltpu.VMEM((harmonics, harmonics), jnp.bfloat16),
            pltpu.VMEM((harmonics, harmonics), jnp.bfloat16),
            pltpu.VMEM((harmonics // block, 2 * block, 2 * columns), jnp.bfloat16),
            pltpu.VMEM((3 * harmonics, 2 * columns), jnp.bfloat16),
            dma((4,)),
            pltpu.SemaphoreType.REGULAR,
            dma((chunks, members)),
            dma((chunks, 2 * reach + 1, inner)),
            dma((chunks, 2 * outer - 1)),
            dma((chunks, 2 * outer - 1, inner)),
            dma((chunks, 2 * reach + 1, inner)),
            dma((1, members)),
            dma((1, 2 * reach + 1, inner)),
            dma((1, 2 * outer - 1)),
            dma((1, 2 * outer - 1, inner)),
        ],
        compiler_params=pltpu.CompilerParams(collective_id=0, has_side_effects=True),
        name="sweep",
    )(source, transfer, fields, orders)
    return (grads * norm_scale)[None], bottom[None]


def solution(mesh):
    return jax.shard_map(
        per_device,
        mesh=mesh,
        in_specs=(
            P(None, "harm", None),
            P("layer", None, "harm", None),
            P("layer", None, "harm", None),
            P(),
        ),
        out_specs=(P("layer", None, "harm"), P("layer", None, "harm", None)),
        check_vma=False,
    )
```

time: 68.7 us -> 61.6 us (0.90)
  the two profiles are of different devices: /device:TPU:0 before, /device:TPU:2 now
where the time goes in v1:
time: 61.6 us; the launch traced here: 61.4 us
  Pallas kernels  57.9 us (94%)
  local copies, waits for them, and re-layouts  1.57 us (3%)
  other arithmetic  1.28 us (2%)
  between operations  0.64 us (1%)
    pallas_call x1, Pallas kernels, per_device(): pl.pallas_call(functools.partial(sweep_kernel, sections, members, inner,...  57.9 us
    unnamed x1, local copies, waits for them, and re-layouts  1.57 us
    broadcast_in_dim x1, other arithmetic, per_device(): return ((grads * norm_scale)[None], bottom[None])  1.28 us

profile of v1, /device:TPU:2, one launch (start us, length us, event | category | flops | bytes accessed | tf_op | source)
XLA Modules:
  0.0 61.4 jit_solution(11571024147108187077)
XLA Ops:
  0.6 57.9 %sweep.1 = (f32[2,512]{1,0:T(2,128)}, bf16[2,256,128]{2,1,0:T(8,128)(2,1)}) custom-call(bf16[2,256,128]{2,1,0:T(8,128)(2,1)} %source_ref.1, bf16[1,2,256,2048]{3,2,1,0:T(8,128)(2,1)} %transfer_ref.1, bf16[1,2,256,128]{3,2,1,0:T(8,128)(2,1)} %fields_ref.1, s32[2048]{0:T(1024)} %orders_ref.1), custom_call_target="tpu_custom_call" | custom-call | tf_op jit(solution)/shard_map/sweep/pallas_call | solution.py:401
  58.5 1.3 %multiply_bitcast_fusion = f32[1,2,512]{2,1,0:T(2,128)} fusion(f32[2,512]{1,0:T(2,128)} %get-tuple-element.4), kind=kLoop, calls=%fused_computation | loop fusion | flops 1024 | bytes 8192 | tf_op jit(solution)/shard_map/broadcast_in_dim | solution.py:434
  59.8 1.6 %copy.7 = bf16[1,2,256,128]{3,2,1,0:T(8,128)(2,1)} copy(bf16[1,2,256,128]{3,2,1,0:T(8,128)(2,1)} %bitcast.3) | data formatting | bytes 262144
